TPU v7x, 32 devices: a whole 2x2x4 slice. The times are simulated.
32 devices in a mesh: groups: 2 (over x), seq: 8 (over z, y), head: 2 (over core).
Axes of the slice: x: 2, y: 2, z: 4, core: 2. Of those that a mesh axis runs over, the one named last changes fastest.
Arguments:
- queries: bfloat16 [4096, 3584], P(('groups', 'seq'), 'head'), parts along dimension 0, may hold values from -30 to 30
- current_keys: bfloat16 [4096, 512], P(('groups', 'seq'), 'head'), parts along dimension 0, may hold values from -6 to 6
- current_values: bfloat16 [4096, 512], P(('groups', 'seq'), 'head'), parts along dimension 0, may hold values from -6 to 6
- stored_keys: bfloat16 [4096, 2, 512], P(('groups', 'seq'), None, 'head'), parts along dimension 0, may hold values from -22 to 22
- stored_values: bfloat16 [4096, 2, 512], P(('groups', 'seq'), None, 'head'), parts along dimension 0, may hold values from -6 to 6
- remap_table: int32 [3, 64], P(None, ('groups', 'seq')), parts along dimension 1, may hold values from 0 to 2047
- block_table: int32 [256], P('groups'), parts along dimension 0, may hold values from 0 to 15, as said below
Outputs:
- attended: bfloat16 [4096, 3584], P(('groups', 'seq'), 'head'), parts along dimension 0
- paged_keys: bfloat16 [4, 256, 2048], P('head', ('groups', 'seq')), parts along dimension 1
- paged_values: bfloat16 [4, 256, 2048], P('head', ('groups', 'seq')), parts along dimension 1
There are 2 independent parts, one for each index of `groups`. A program takes and returns all parts, laid end to end along the dimension named above; each array names one. Nothing has to cross between parts.
Inputs may be any that keep to these rules, and one draw needn't show every extreme that they name: `block_table`: the entries of the blocks b that share b modulo 8 are a permutation of 0 to 15.
All inputs are finite; a program needn't handle non-finite values.
Results may differ from a plain program's by a relative error of at most 0.012.
The roundings to bfloat16 on the way count: a program that leaves them out, or rounds other values in their place, can miss the bound.
Values may be sent and summed in bfloat16 or wider, within the bound.
A program may use at most 128 MiB of HBM per device.

v0:
```python
import functools
import math

import jax
import jax.numpy as jnp
from jax import lax
from jax.experimental import pallas as pl
from jax.experimental.pallas import tpu as pltpu
from jax.sharding import PartitionSpec as P

HEAD_SIZE = 128
PRIOR_SEGMENTS = 2
PAGE_TOKENS = 16
QBLK = 64
KINDS = PRIOR_SEGMENTS + 1
OWN_PART = PRIOR_SEGMENTS

rope_base = 1000000.0
masked_value = -1e30
MESH = pl.DeviceIdType.MESH
RIGHT, LEFT, ACROSS = 0, 1, 2


def kernel(
    n, kv_local, per_group, q_hbm, cos_ref, sin_ref, stored_ref, keys_hbm, values_hbm,
    out_ref, raw_ref, q_ref, held, turned, top, denom, total, own_sem, send_sem, recv_sem,
):
    me = lax.axis_index("seq")
    partner = me + 1 - 2 * (me % 2)
    tokens = q_hbm.shape[0]
    heads = kv_local * per_group
    scale = HEAD_SIZE ** -0.5 * math.log2(math.e)
    has_right = me + 2 < n
    has_left = me - 2 >= 0

    own = [
        pltpu.make_async_copy(stored_ref, held.at[me, pl.ds(0, PRIOR_SEGMENTS)], own_sem.at[0]),
        pltpu.make_async_copy(keys_hbm, held.at[me, OWN_PART, 0], own_sem.at[1]),
        pltpu.make_async_copy(values_hbm, held.at[me, OWN_PART, 1], own_sem.at[2]),
        pltpu.make_async_copy(q_hbm, q_ref, own_sem.at[3]),
    ]
    for copy in own:
        copy.start()
    barrier = pltpu.get_barrier_semaphore()
    pl.semaphore_signal(barrier, inc=1, device_id={"seq": partner}, device_id_type=MESH)

    @pl.when(has_right)
    def _():
        pl.semaphore_signal(barrier, inc=1, device_id={"seq": me + 2}, device_id_type=MESH)

    @pl.when(has_left)
    def _():
        pl.semaphore_signal(barrier, inc=1, device_id={"seq": me - 2}, device_id_type=MESH)

    expected = 1 + has_right.astype(jnp.int32) + has_left.astype(jnp.int32)
    pl.semaphore_wait(barrier, expected)
    for copy in own[:3]:
        copy.wait()

    def remote(way, j, part):
        target = (me + 2, me - 2, partner)[way]
        return pltpu.make_async_remote_copy(
            src_ref=held.at[j, part],
            dst_ref=held.at[j, part],
            send_sem=send_sem.at[way, j, part],
            recv_sem=recv_sem.at[j, part],
            device_id={"seq": target},
            device_id_type=MESH,
        )

    def goes(way, j, part):
        mine = (j % 2) == (me % 2)
        stored = part < PRIOR_SEGMENTS
        if way == RIGHT:
            relayed = (j == partner) & (part == 0) & (me + 4 >= n)
            return ((mine & (j <= me)) | relayed) & has_right
        if way == LEFT:
            return mine & (j >= me) & stored & has_left
        relayed = (j == me - 2) & (part == 0) & (me + 2 >= n)
        return mine & (stored | (j <= partner)) & jnp.logical_not(relayed)

    def forward(j, part):
        for way in (ACROSS, RIGHT, LEFT):

            @pl.when(goes(way, j, part))
            def _():
                remote(way, j, part).start()

    for part in range(KINDS):
        forward(me, part)
    own[3].wait()

    def turn(part, carry):
        cos = cos_ref[part]
        sin = sin_ref[part]
        for h in range(heads):
            x = q_ref[:, h * HEAD_SIZE : (h + 1) * HEAD_SIZE].astype(jnp.float32)
            y = x * cos + pltpu.roll(x, HEAD_SIZE // 2, 1) * sin
            turned[part, h] = y.T.astype(jnp.bfloat16)
        return carry

    lax.fori_loop(0, KINDS, turn, 0)
    top[...] = jnp.full(top.shape, masked_value, jnp.float32)
    denom[...] = jnp.zeros(denom.shape, jnp.float32)
    total[...] = jnp.zeros(total.shape, jnp.float32)

    def absorb(j, part, causal):
        keys = [held[j, part, 0, :, g * HEAD_SIZE : (g + 1) * HEAD_SIZE] for g in range(kv_local)]
        values = [
            held[j, part, 1, :, g * HEAD_SIZE : (g + 1) * HEAD_SIZE].T for g in range(kv_local)
        ]

        def score(h):
            return jnp.dot(
                keys[h // per_group], turned[part, h], preferred_element_type=jnp.float32
            )

        def add(h, weights, factor):
            total[h] = total[h] * factor + jnp.dot(
                values[h // per_group], weights, preferred_element_type=jnp.float32
            )

        pending = None
        following = score(0)
        for h in range(heads):
            scores = following
            if h + 1 < heads:
                following = score(h + 1)
            if causal:
                key_index = lax.broadcasted_iota(jnp.int32, scores.shape, 0)
                row_index = lax.broadcasted_iota(jnp.int32, scores.shape, 1)
                scores = jnp.where(key_index <= row_index, scores, masked_value)
            old = top[h]
            new = jnp.maximum(old, jnp.max(scores, 0, keepdims=True))
            factor = jnp.exp2((old - new) * scale)
            weights = jnp.exp2((scores - new) * scale)
            top[h] = new
            denom[h] = denom[h] * factor + jnp.sum(weights, 0, keepdims=True)
            if pending is not None:
                add(*pending)
            pending = (h, weights.astype(jnp.bfloat16), factor)
        add(*pending)

    def own_step(part, carry):
        absorb(me, part, False)
        return carry

    lax.fori_loop(0, PRIOR_SEGMENTS, own_step, 0)
    absorb(me, OWN_PART, True)

    def round_step(step, carry):
        distance = step // (4 * KINDS) + 1
        part = (step // 4) % KINDS
        kind = step % 4
        near = distance - kind // 2
        start = jnp.where(kind < 2, me, partner)
        sign = 1 - 2 * (kind % 2)
        j = start - sign * 2 * near
        stored = part < PRIOR_SEGMENTS
        wanted = (j >= 0) & (j < n) & (stored | (j <= me)) & ((near > 0) | (kind % 2 == 0))

        @pl.when(wanted)
        def _():
            remote(RIGHT, j, part).wait_recv()
            forward(j, part)
            absorb(j, part, False)

        return carry

    lax.fori_loop(0, (n // 2) * 4 * KINDS, round_step, 0)

    rounds = tokens // PAGE_TOKENS // n
    last = PRIOR_SEGMENTS - 1

    def page_step(j, carry):
        for r in range(rounds):
            rows = pl.ds(pl.multiple_of((r * n + me) * PAGE_TOKENS, PAGE_TOKENS), PAGE_TOKENS)
            for which in range(2):
                raw_ref[which, j * rounds + r] = held[j, last, which, rows, :]
        return carry

    lax.fori_loop(0, n, page_step, 0)

    for h in range(heads):
        finished = total[h] / denom[h]
        out_ref[:, h * HEAD_SIZE : (h + 1) * HEAD_SIZE] = finished.T.astype(out_ref.dtype)

    def drain(step, carry):
        j = step // KINDS
        part = step % KINDS
        for way in (ACROSS, RIGHT, LEFT):

            @pl.when(goes(way, j, part))
            def _():
                remote(way, j, part).wait_send()

        return carry

    lax.fori_loop(0, n * KINDS, drain, 0)


def shards(
    queries, current_keys, current_values, stored_keys, stored_values, remap_table, block_table
):
    tokens, width = queries.shape
    key_width = current_keys.shape[1]
    kv_local = key_width // HEAD_SIZE
    heads = width // HEAD_SIZE
    per_group = heads // kv_local
    my_index = lax.axis_index("seq")
    owners = lax.axis_size("seq")
    positions = (
        jnp.repeat(remap_table, QBLK, axis=1)
        + (jnp.arange(tokens, dtype=jnp.int32) % QBLK)[None, :]
    )
    positions = jnp.stack([positions[2], positions[1], positions[0]])
    half_dim = HEAD_SIZE // 2
    frequency = rope_base ** (-2.0 * jnp.arange(half_dim, dtype=jnp.float32) / HEAD_SIZE)
    angles = positions.astype(jnp.float32)[..., None] * frequency
    cos = jnp.cos(angles)
    sin = jnp.sin(angles)
    cos = jnp.concatenate([cos, cos], -1)
    sin = jnp.concatenate([-sin, sin], -1)
    stored = jnp.stack(
        [
            jnp.stack([stored_keys[:, s, :], stored_values[:, s, :]])
            for s in range(PRIOR_SEGMENTS)
        ]
    )
    rounds = tokens // PAGE_TOKENS // owners
    hbm = pl.BlockSpec(memory_space=pltpu.HBM)
    vmem = pl.BlockSpec(memory_space=pltpu.VMEM)
    attended, raw = pl.pallas_call(
        functools.partial(kernel, owners, kv_local, per_group),
        out_shape=(
            jax.ShapeDtypeStruct((tokens, width), jnp.bfloat16),
            jax.ShapeDtypeStruct((2, owners * rounds, PAGE_TOKENS, key_width), jnp.bfloat16),
        ),
        in_specs=[hbm, vmem, vmem, vmem, hbm, hbm],
        out_specs=(vmem, vmem),
        scratch_shapes=[
            pltpu.VMEM((tokens, width), jnp.bfloat16),
            pltpu.VMEM((owners, KINDS, 2, tokens, key_width), jnp.bfloat16),
            pltpu.VMEM((KINDS, heads, HEAD_SIZE, tokens), jnp.bfloat16),
            pltpu.VMEM((heads, 1, tokens), jnp.float32),
            pltpu.VMEM((heads, 1, tokens), jnp.float32),
            pltpu.VMEM((heads, HEAD_SIZE, tokens), jnp.float32),
            pltpu.SemaphoreType.DMA((4,)),
            pltpu.SemaphoreType.DMA((3, owners, KINDS)),
            pltpu.SemaphoreType.DMA((owners, KINDS)),
        ],
        compiler_params=pltpu.CompilerParams(
            collective_id=0, has_side_effects=True, vmem_limit_bytes=48 * 1024 * 1024
        ),
    )(queries, cos, sin, stored, current_keys, current_values)
    pages_here = owners * rounds
    arranged = (
        raw.reshape(2, pages_here, PAGE_TOKENS, kv_local, HEAD_SIZE)
        .transpose(0, 3, 1, 2, 4)
        .reshape(2, kv_local, pages_here, PAGE_TOKENS * HEAD_SIZE)
    )
    source_index = jnp.arange(owners, dtype=jnp.int32)[:, None]
    round_index = jnp.arange(rounds, dtype=jnp.int32)[None, :]
    block_index = source_index * (tokens // PAGE_TOKENS) + round_index * owners + my_index
    target = block_table[block_index.reshape(-1)]
    paged = jnp.zeros_like(arranged).at[:, :, target].set(arranged)
    return (attended, paged[0], paged[1])


def solution(mesh):
    in_specs = (
        P(("groups", "seq"), "head"),
        P(("groups", "seq"), "head"),
        P(("groups", "seq"), "head"),
        P(("groups", "seq"), None, "head"),
        P(("groups", "seq"), None, "head"),
        P(None, ("groups", "seq")),
        P("groups"),
    )
    out_specs = (
        P(("groups", "seq"), "head"),
        P("head", ("groups", "seq"), None),
        P("head", ("groups", "seq"), None),
    )
    return jax.shard_map(shards, mesh=mesh, in_specs=in_specs, out_specs=out_specs, check_vma=False)
```

profile of v0, /device:TPU:28, one launch (start us, length us, event | category | flops | bytes accessed | tf_op | source)
XLA Modules:
  0.0 83.6 jit_solution(13449705539443444670)
XLA Ops:
  0.6 0.0 copy-start
  0.6 0.8 broadcast_in_dim.4
  1.4 0.1 reshape.109
  1.5 1.4 %fusion = (f32[3,256,64]{2,1,0:T(8,128)S(1)}, f32[3,256,64]{2,1,0:T(8,128)S(1)}, f32[3,256,64]{2,1,0:T(8,128)S(1)}) fusion(f32[64]{0:T(128)S(1)} %multiply_power_fusion, f32[3,256]{1,0:T(4,128)S(1)} %add_convert_fusion), kind=kLoop, calls=%fused_computation.15 | loop fusion | flops 98304 | bytes 593152 | tf_op jit(solution)/shard_map/neg | solution.py:223
  3.0 0.3 pad_maximum_fusion.1
  3.3 0.7 copy-done.4
  3.9 0.4 fusion.4
  4.4 0.9 %copy-done.5 = bf16[256,2,256]{2,1,0:T(2,128)(2,1)S(1)} copy-done((bf16[256,2,256]{2,1,0:T(2,128)(2,1)S(1)}, bf16[256,2,256]{2,1,0:T(2,128)(2,1)}, u32[]{:S(2)}) %copy-start.5) | copy-done | bytes 262168
  5.3 0.4 fusion.3
  5.8 0.1 pad_maximum_fusion.stored_ref
  5.8 1.1 %copy-done.1 = bf16[256,1792]{1,0:T(8,128)(2,1)S(1)} copy-done((bf16[256,1792]{1,0:T(8,128)(2,1)S(1)}, bf16[256,1792]{1,0:T(8,128)(2,1)}, u32[]{:S(2)}) %copy-start.1) | copy-done | bytes 917528
  6.9 0.0 copy-done.3
  6.9 71.6 %shard_map.94 = (bf16[256,1792]{1,0:T(8,128)(2,1)S(1)}, bf16[2,16,16,256]{3,2,1,0:T(8,128)(2,1)S(1)}) custom-call(bf16[256,1792]{1,0:T(8,128)(2,1)S(1)} %copy-done.1, f32[3,256,128]{2,1,0:T(8,128)S(1)} %get-tuple-element.25.cos_ref, f32[3,256,128]{2,1,0:T(8,128)S(1)} %get-tuple-element.26.sin_ref, bf16[2,2,256,256]{3,2,1,0:T(8,128)(2,1)S(1)} %pad_maximum_fusion.stored_ref, ...), custom_call_target="tpu_custom_call" | custom-call | tf_op jit(solution)/shard_map/pallas_call | solution.py:233
  78.6 0.1 reshape.110
  78.7 0.1 reshape.121
  78.8 0.1 add_add_fusion
  78.9 0.1 add.85
  79.0 0.7 gather_fusion
  79.7 0.1 broadcast_in_dim.5
  79.8 1.2 %scatter_fusion = bf16[2,2,16,2048]{3,1,2,0:T(2,128)(2,1)S(1)} fusion(bf16[2,2,16,2048]{3,1,2,0:T(2,128)(2,1)S(1)} %broadcast_in_dim.5, s32[16]{0:T(128)S(1)} %fusion.2, bf16[16,2,2,2048]{3,2,1,0:T(2,128)(2,1)S(1)} %bitcast.31), kind=kCustom, calls=%fused_computation.1 | custom fusion | bytes 786496 | tf_op jit(solution)/shard_map/scatter | solution.py:266
  81.1 0.2 slice_bitcast_fusion
  81.2 0.7 copy.22
  81.9 0.7 copy.23
  82.6 0.9 %copy.34 = bf16[256,1792]{1,0:T(8,128)(2,1)} copy(bf16[256,1792]{1,0:T(8,128)(2,1)S(1)} %get-tuple-element.34) | data formatting | bytes 1835008
  (22 shorter events, 0.3 us)
Async XLA Ops:
  0.6 78.4 %copy-start = (s32[128]{0:T(128)S(1)}, s32[128]{0:T(128)}, u32[]{:S(2)}) copy-start(s32[128]{0:T(128)} %param.13) | copy-start | bytes 1540
  3.0 1.0 %copy-start.4 = (bf16[256,2,256]{2,1,0:T(2,128)(2,1)S(1)}, bf16[256,2,256]{2,1,0:T(2,128)(2,1)}, u32[]{:S(2)}) copy-start(bf16[256,2,256]{2,1,0:T(2,128)(2,1)} %param.11) | copy-start | bytes 786436
  4.3 1.0 %copy-start.5 = (bf16[256,2,256]{2,1,0:T(2,128)(2,1)S(1)}, bf16[256,2,256]{2,1,0:T(2,128)(2,1)}, u32[]{:S(2)}) copy-start(bf16[256,2,256]{2,1,0:T(2,128)(2,1)} %param.10) | copy-start | bytes 786436
  5.7 1.2 %copy-start.1 = (bf16[256,1792]{1,0:T(8,128)(2,1)S(1)}, bf16[256,1792]{1,0:T(8,128)(2,1)}, u32[]{:S(2)}) copy-start(bf16[256,1792]{1,0:T(8,128)(2,1)} %q_hbm.1) | copy-start | bytes 2752516
  5.8 1.1 %copy-start.2 = (bf16[256,256]{1,0:T(8,128)(2,1)S(1)}, bf16[256,256]{1,0:T(8,128)(2,1)}, u32[]{:S(2)}) copy-start(bf16[256,256]{1,0:T(8,128)(2,1)} %keys_hbm.1) | copy-start | bytes 393220
  5.8 1.2 %copy-start.3 = (bf16[256,256]{1,0:T(8,128)(2,1)S(1)}, bf16[256,256]{1,0:T(8,128)(2,1)}, u32[]{:S(2)}) copy-start(bf16[256,256]{1,0:T(8,128)(2,1)} %values_hbm.1) | copy-start | bytes 393220
where the time goes:
time: 83.8 us; the launch traced here: 83.6 us
  Pallas kernels  71.6 us (85%)
  local copies, waits for them, and re-layouts  9.14 us (11%)
  other arithmetic  1.96 us (2%)
    pallas_call x1, Pallas kernels, shards(): pl.pallas_call(functools.partial(kernel, owners, kv_local, per_group), ou...  71.6 us
    unnamed x15, local copies, waits for them, and re-layouts  5 us

commit v1 on v0

v1 whole, which is shorter than its diff:
```python
import functools
import heapq
import math

import jax
import jax.numpy as jnp
from jax import lax
from jax.experimental import pallas as pl
from jax.experimental.pallas import tpu as pltpu
from jax.sharding import PartitionSpec as P

HEAD_SIZE = 128
PRIOR_SEGMENTS = 2
PAGE_TOKENS = 16
QBLK = 64
KINDS = PRIOR_SEGMENTS + 1
CURRENT = PRIOR_SEGMENTS

rope_base = 1000000.0
masked_value = -1e30
MESH = pl.DeviceIdType.MESH
RIGHT, LEFT, ACROSS = 0, 1, 2
ONES_ROWS = 16

OWN0, OWN1, GUEST, SPARE = 0, 1, 2, 3
NOTHING, BATCH2, BATCH1, TURN, DIAGONAL, GUEST_TURN, PACK, RETURN, PAGES, MERGE = range(10)
FIELD = 128

WIRE, HOP, RELAY = 2.81, 1.9, 1.0
COST = {BATCH2: 2.6, BATCH1: 1.5, TURN: 4.0, DIAGONAL: 1.6, GUEST_TURN: 2.0, PACK: 0.8, PAGES: 1.3}


def offloaded(n, d):
    if d < n - 2 or n < 4:
        return set()
    return {
        (j, part, 0)
        for j in range(n - 2)
        for part in (0, CURRENT)
        if part < CURRENT or j <= n - 4
    }


def needed(n, groups, d):
    left = offloaded(n, d)
    return {
        (j, part, g)
        for j in range(n)
        for part in range(KINDS)
        for g in range(groups)
        if j != d and (part < CURRENT or j < d) and (j, part, g) not in left
    }


def route(n, groups):
    need = {d: needed(n, groups, d) for d in range(n)}
    here = {
        d: {(d, part, g): 0.0 for part in range(KINDS) for g in range(groups)} for d in range(n)
    }
    taken = {d: set(here[d]) for d in range(n)}
    lack = {}
    for d in range(n):
        for x in sorted(need[d]):
            lack[x] = lack.get(x, 0) + 1
    target = {}
    for d in range(n):
        if d + 2 < n:
            target[(d, RIGHT)] = d + 2
        if d - 2 >= 0:
            target[(d, LEFT)] = d - 2
        target[(d, ACROSS)] = d ^ 1
    wanted = {d - 2: offloaded(n, d) for d in range(n) if offloaded(n, d)}
    urgent = set().union(*wanted.values()) if wanted else set()
    free = {link: 0.0 for link in target}
    for h in wanted:
        free[(h + 2, LEFT)] = 3.5 * WIRE
    ready = {}
    returned = {}
    sends = {link: [] for link in target}
    arrivals = {d: {} for d in range(n)}
    events = []
    for k, link in enumerate(target):
        heapq.heappush(events, (free[link], k, 0, link))
    count = len(events)
    idle = set()

    def pick(link, now):
        u, v = link[0], target[link]
        if link[1] == RIGHT and u in wanted and u not in returned and ready.get(u, now + 1) <= now:
            return RETURN
        best = None
        for x in sorted(here[u]):
            if here[u][x] > now + 1e-9 or x in taken[v] or x not in need[v]:
                continue
            others = sum(1 for w in (v + 2, v - 2, v ^ 1) if 0 <= w < n and w != u and x in taken[w])
            score = lack[x] - SHARED * others
            if x in urgent and (v in wanted or (link[1] != LEFT and v < n - 4)):
                score += BONUS
            score += ((x[0] * 7 + x[1] * 5 + x[2] * 3 + u * 11 + link[1] * 13 + SALT) * 7919 % 101) / 101
            if best is None or score > best[0]:
                best = (score, x)
        return None if best is None else best[1]

    while events:
        now, _, kind, what = heapq.heappop(events)
        if kind == 0:
            link = what
            if free[link] > now + 1e-9:
                heapq.heappush(events, (free[link], count, 0, link))
                count += 1
                continue
            x = pick(link, now)
            if x is None:
                idle.add(link)
                continue
            v = target[link]
            if x == RETURN:
                returned[link[0]] = now + 3.6 * WIRE + HOP
                free[link] = now + 3.6 * WIRE
            else:
                taken[v].add(x)
                lack[x] -= 1
                sends[link].append(x)
                arrivals[v][x] = now + WIRE + HOP
                here[v][x] = now + WIRE + HOP + RELAY
                free[link] = now + WIRE
                heapq.heappush(events, (here[v][x], count, 1, v))
                count += 1
                if v in wanted and v not in ready and wanted[v] <= set(here[v]):
                    ready[v] = max(here[v][y] for y in wanted[v]) + 4.0
                    heapq.heappush(events, (ready[v], count, 1, v))
                    count += 1
            heapq.heappush(events, (free[link], count, 0, link))
            count += 1
        else:
            for link in sorted(x for x in idle if x[0] == what):
                idle.discard(link)
                heapq.heappush(events, (max(now, free[link]), count, 0, link))
                count += 1
    return sends, arrivals, wanted, returned


SALT, BONUS, SHARED = 16, 3.0, 2.0


def schedule(n, groups):
    sends, arrivals, wanted, returned = route(n, groups)
    tables = []
    for d in range(n):
        rows = []
        have = {(d, part, g) for part in range(KINDS) for g in range(groups)}
        queue = {way: list(sends.get((d, way), [])) for way in (RIGHT, LEFT, ACROSS)}
        order = sorted(arrivals[d], key=lambda x: (arrivals[d][x], x))
        guest = sorted(wanted.get(d, ()))
        pending = {OWN0: [], OWN1: [], GUEST: []}
        absorbed_guest = 0
        turned_guest = packed = sent_back = paged = False
        pages_left = {(j, 1, g) for j in range(n) for g in range(groups)} - have

        def ready_sends():
            out = {}
            for way, q in queue.items():
                if q and q[0] in have:
                    out[way] = q.pop(0)
            return out

        def emit(wait=None, op=NOTHING, pieces=(), accs=()):
            if wait is not None:
                have.add(wait)
            rows.append([wait, ready_sends(), op, list(pieces), list(accs)])
            while True:
                more = ready_sends()
                if not more:
                    break
                rows.append([None, more, NOTHING, [], []])

        def note(x):
            pages_left.discard(x)
            pending[x[2]].append(x)
            if x in guest:
                pending[GUEST].append(x)

        def streams(count, size):
            chosen = []
            for acc in (GUEST, OWN0, OWN1):
                if acc == GUEST and not turned_guest:
                    continue
                while len(pending[acc]) >= size and len(chosen) < count:
                    chosen.append((acc, [pending[acc].pop(0) for _ in range(size)]))
            return chosen

        def put_back(chosen):
            for acc, pieces in reversed(chosen):
                pending[acc] = pieces + pending[acc]

        def batch(op, chosen):
            nonlocal now, absorbed_guest
            pieces, accs = [], []
            for acc, some in chosen:
                pieces += some
                accs.append(acc)
                absorbed_guest += len(some) if acc == GUEST else 0
            emit(None, op, pieces, accs)
            now += COST[op]

        emit()
        emit(None, TURN)
        now = COST[TURN]
        for g in range(groups):
            for part in range(PRIOR_SEGMENTS):
                note((d, part, g))
            if (d, CURRENT, g) in guest:
                pending[GUEST].append((d, CURRENT, g))
        first = [(OWN0, [pending[OWN0].pop(0) for _ in range(2)]),
                 (OWN1, [pending[OWN1].pop(0) for _ in range(2)])]
        batch(BATCH2, first)
        emit(None, DIAGONAL)
        now += COST[DIAGONAL]
        guest_at = 3.5 * WIRE + HOP + 1.0
        while True:
            while order and arrivals[d][order[0]] <= now + 0.2:
                x = order.pop(0)
                emit(x)
                note(x)
            if guest and not turned_guest and guest_at <= now:
                emit(None, GUEST_TURN)
                now += COST[GUEST_TURN]
                turned_guest = True
                continue
            if packed and not sent_back:
                emit(None, RETURN)
                sent_back = True
                continue
            if guest and not packed and absorbed_guest == len(guest):
                emit(None, PACK)
                now += COST[PACK]
                packed = True
                continue
            chosen = streams(2, 2)
            if len(chosen) == 2:
                batch(BATCH2, chosen)
                continue
            put_back(chosen)
            last_guest = (
                guest and turned_guest and absorbed_guest + len(pending[GUEST]) == len(guest)
            )
            upcoming = arrivals[d][order[0]] if order else None
            if last_guest and pending[GUEST]:
                chosen = streams(2, 1)
                if len(chosen) == 1:
                    chosen.append((SPARE, list(chosen[0][1])))
                batch(BATCH1, chosen)
                continue
            if not pages_left and not paged:
                emit(None, PAGES)
                now += COST[PAGES]
                paged = True
                continue
            if guest and not turned_guest and (upcoming is None or guest_at <= upcoming):
                now = max(now, guest_at)
                continue
            if upcoming is None or upcoming - now > 1.2:
                chosen = streams(2, 1)
                if len(chosen) == 2:
                    batch(BATCH1, chosen)
                    continue
                if chosen and upcoming is None:
                    chosen.append((SPARE, list(chosen[0][1])))
                    batch(BATCH1, chosen)
                    continue
                put_back(chosen)
            if upcoming is None:
                break
            now = max(now, upcoming)
        if offloaded(n, d):
            emit(None, MERGE)
        assert not any(queue.values()) and not any(pending.values()) and paged
        tables.append(rows)
    length = max(len(rows) for rows in tables)

    def number(x):
        return (x[0] * KINDS + x[1]) * groups + x[2]

    packed_tables = []
    for rows in tables:
        words = []
        for wait, sent, op, pieces, accs in rows:
            first = 0 if wait is None else number(wait) + 1
            for way in (RIGHT, LEFT, ACROSS):
                if way in sent:
                    first += (number(sent[way]) + 1) * FIELD ** (way + 1)
            second = sum(number(x) * FIELD**k for k, x in enumerate(pieces))
            third = op + 16 * sum(acc * 4**k for k, acc in enumerate(accs))
            words.append((first, second, third))
        words += [(0, 0, 0)] * (length - len(words))
        packed_tables.append(words)
    return length, packed_tables


def kernel(
    n, groups, per_group, length, tables,
    table_ref, turns_ref, freq_ref, q_hbm, stored_ref, keys_hbm, values_hbm,
    out_ref, paged_ref,
    rows_ref, q_ref, guest_q, guest_turns, cos_ref, sin_ref, held, turned, top, total, raw,
    back, back_stats, came, came_stats, own_sem, send_sem, recv_sem, side_send, side_recv,
):
    me = lax.axis_index("seq")
    partner = me + 1 - 2 * (me % 2)
    tokens = q_hbm.shape[0]
    heads = groups * per_group
    blocks = tokens // QBLK
    scale = HEAD_SIZE ** -0.5 * math.log2(math.e)
    has_right = me + 2 < n
    has_left = me - 2 >= 0
    is_top = me >= n - 2
    is_helper = (me >= n - 4) & (me < n - 2)
    width = per_group * HEAD_SIZE

    def at(j, part, g):
        return (j * KINDS + part) * groups + g

    own = [pltpu.make_async_copy(q_hbm, q_ref, own_sem.at[0])]
    for part in range(PRIOR_SEGMENTS):
        for g in range(groups):
            own.append(
                pltpu.make_async_copy(
                    stored_ref.at[part, g], held.at[at(me, part, g)], own_sem.at[len(own)]
                )
            )
    for g in range(groups):
        for kv, ref in enumerate((keys_hbm, values_hbm)):
            own.append(
                pltpu.make_async_copy(
                    ref.at[:, pl.ds(g * HEAD_SIZE, HEAD_SIZE)],
                    held.at[at(me, CURRENT, g), kv],
                    own_sem.at[len(own)],
                )
            )
    for copy in own:
        copy.start()
    barrier = pltpu.get_barrier_semaphore()
    pl.semaphore_signal(barrier, inc=1, device_id={"seq": partner}, device_id_type=MESH)

    @pl.when(has_right)
    def _():
        pl.semaphore_signal(barrier, inc=1, device_id={"seq": me + 2}, device_id_type=MESH)

    @pl.when(has_left)
    def _():
        pl.semaphore_signal(barrier, inc=1, device_id={"seq": me - 2}, device_id_type=MESH)

    for d in range(n):

        @pl.when(me == d)
        def _():
            for k, words in enumerate(tables[d]):
                rows_ref[0, k] = words[0]
                rows_ref[1, k] = words[2]

    expected = 1 + has_right.astype(jnp.int32) + has_left.astype(jnp.int32)
    pl.semaphore_wait(barrier, expected)

    def side(index, source, destination, target):
        return pltpu.make_async_remote_copy(
            src_ref=source,
            dst_ref=destination,
            send_sem=side_send.at[index],
            recv_sem=side_recv.at[index],
            device_id={"seq": target},
            device_id_type=MESH,
        )

    down = jnp.maximum(me - 2, 0)
    up = jnp.minimum(me + 2, n - 1)
    send_q = side(0, q_ref.at[:, pl.ds(0, width)], guest_q, down)
    send_turns = side(1, turns_ref, guest_turns, down)
    send_back = side(2, back, came, up)
    send_stats = side(3, back_stats, came_stats, up)

    own[0].wait()

    @pl.when(is_top)
    def _():
        send_turns.start()
        send_q.start()

    for copy in own[1:]:
        copy.wait()

    def remote(way, piece):
        target = (me + 2, me - 2, partner)[way]
        return pltpu.make_async_remote_copy(
            src_ref=held.at[piece],
            dst_ref=held.at[piece],
            send_sem=send_sem.at[way, piece],
            recv_sem=recv_sem.at[piece],
            device_id={"seq": target},
            device_id_type=MESH,
        )

    def fields(row):
        word = rows_ref[0, row]
        return [word // FIELD**k % FIELD for k in range(4)]

    def tables_of(ref):
        rows = lax.broadcasted_iota(jnp.int32, (QBLK, HEAD_SIZE), 0).astype(jnp.float32)
        angle = rows * freq_ref[...]
        near_cos, near_sin = jnp.cos(angle), jnp.sin(angle)
        far = ref[...]
        far_cos, far_sin = jnp.cos(far), jnp.sin(far)
        lane = lax.broadcasted_iota(jnp.int32, (QBLK, HEAD_SIZE), 1)
        for part in range(KINDS):
            for b in range(blocks):
                r = part * blocks + b
                c, s = far_cos[r : r + 1], far_sin[r : r + 1]
                span = slice(b * QBLK, (b + 1) * QBLK)
                cos_ref[part, span] = c * near_cos - s * near_sin
                sin = s * near_cos + c * near_sin
                sin_ref[part, span] = jnp.where(lane < HEAD_SIZE // 2, -sin, sin)

    def turn(source, count, base):
        def one(part, carry):
            cos = cos_ref[part]
            sin = sin_ref[part]
            for h in range(count):
                x = source[:, h * HEAD_SIZE : (h + 1) * HEAD_SIZE].astype(jnp.float32)
                y = x * cos + pltpu.roll(x, HEAD_SIZE // 2, 1) * sin
                y = y.astype(jnp.bfloat16).astype(jnp.float32) * scale
                high = y.astype(jnp.bfloat16)
                low = (y - high.astype(jnp.float32)).astype(jnp.bfloat16)
                turned[part, base + h, :HEAD_SIZE] = high.T
                turned[part, base + h, HEAD_SIZE:] = low.T
            return carry

        lax.fori_loop(0, KINDS, one, 0)

    top[...] = jnp.full(top.shape, masked_value, jnp.float32)

    def clear(h, carry):
        total[h] = jnp.zeros(total.shape[1:], jnp.float32)
        return carry

    lax.fori_loop(0, total.shape[0], clear, 0)

    def absorb(streams, causal=False):
        ready = []
        for pieces, base, query in streams:
            keys = []
            for piece in pieces:
                k = held[piece, 0]
                keys.append((jnp.concatenate([k, k], 1), piece // groups % KINDS))
            values = jnp.concatenate([held[piece, 1] for piece in pieces], 0).T
            ones = jnp.ones((ONES_ROWS, values.shape[1]), jnp.bfloat16)
            ready.append((keys, jnp.concatenate([values, ones], 0), base, query))
        units = [(stream, h) for stream in ready for h in range(per_group)]

        def score(unit):
            (keys, _, _, query), h = unit
            some = [
                jnp.dot(k, turned[part, query + h], preferred_element_type=jnp.float32)
                for k, part in keys
            ]
            return some[0] if len(some) == 1 else jnp.concatenate(some, 0)

        def add(unit, weights, factor):
            (_, values, base, _), h = unit
            total[base + h] = total[base + h] * factor + jnp.dot(
                values, weights, preferred_element_type=jnp.float32
            )

        pending = []
        following = score(units[0])
        for k, unit in enumerate(units):
            scores = following
            if k + 1 < len(units):
                following = score(units[k + 1])
            if causal:
                key_index = lax.broadcasted_iota(jnp.int32, scores.shape, 0)
                row_index = lax.broadcasted_iota(jnp.int32, scores.shape, 1)
                scores = jnp.where(key_index <= row_index, scores, masked_value)
            (_, _, base, _), h = unit
            old = top[base + h]
            new = jnp.maximum(old, jnp.max(scores, 0, keepdims=True))
            factor = jnp.exp2(old - new)
            weights = jnp.exp2(scores - new).astype(jnp.bfloat16)
            top[base + h] = new
            if len(pending) == 2:
                add(*pending.pop(0))
            pending.append((unit, weights, factor))
        for some in pending:
            add(*some)

    rounds = tokens // PAGE_TOKENS // n
    here = n * rounds
    last = PRIOR_SEGMENTS - 1

    def pages():
        def collect(j, carry):
            for r in range(rounds):
                rows = pl.ds(pl.multiple_of((r * n + me) * PAGE_TOKENS, PAGE_TOKENS), PAGE_TOKENS)
                to = pl.ds(pl.multiple_of((j * rounds + r) * PAGE_TOKENS, PAGE_TOKENS), PAGE_TOKENS)
                for kv in range(2):
                    for g in range(groups):
                        raw[kv, to, g * HEAD_SIZE : (g + 1) * HEAD_SIZE] = held[
                            at(j, last, g), kv, rows, :
                        ]
            return carry

        lax.fori_loop(0, n, collect, 0)
        size = here * PAGE_TOKENS
        row = lax.broadcasted_iota(jnp.int32, (size, size), 0)
        column = lax.broadcasted_iota(jnp.int32, (size, size), 1)
        slot = lax.broadcasted_iota(jnp.int32, (1, size), 1) // PAGE_TOKENS
        page = jnp.zeros((1, size), jnp.int32)
        for k in range(here):
            j, r = k // rounds, k % rounds
            entry = table_ref[j * (tokens // PAGE_TOKENS) + r * n + me]
            page = jnp.where(slot == k, entry, page)
        chosen = (row % here == page) & (row // here == column % PAGE_TOKENS)
        pick = jnp.where(chosen, 1.0, 0.0).astype(jnp.bfloat16)
        for kv in range(2):
            moved = jnp.dot(pick, raw[kv], preferred_element_type=jnp.float32)
            moved = moved.astype(jnp.bfloat16)
            for g in range(groups):
                for t in range(PAGE_TOKENS):
                    paged_ref[kv, g, :, t * HEAD_SIZE : (t + 1) * HEAD_SIZE] = moved[
                        t * here : (t + 1) * here, g * HEAD_SIZE : (g + 1) * HEAD_SIZE
                    ]

    guest_base = heads
    spare_base = heads + per_group

    def step(row, carry):
        wait, *sent = fields(row)

        @pl.when(wait > 0)
        def _():
            remote(RIGHT, wait - 1).wait_recv()

        for way in (ACROSS, RIGHT, LEFT):

            @pl.when(sent[way] > 0)
            def _():
                remote(way, sent[way] - 1).start()

        third = rows_ref[1, row]
        op = third % 16

        def listed():
            word = jnp.int32(0)
            for r in range(length):
                choice = None
                for d in range(n):
                    value = tables[d][r][1]
                    if value:
                        choice = value if choice is None else jnp.where(me == d, value, choice)
                if choice is not None:
                    word = jnp.where(row == r, choice, word)
            return word

        def stream(k, size, second):
            acc = third // (16 * 4**k) % 4
            pieces = [second // FIELD ** (k * size + i) % FIELD for i in range(size)]
            base = acc * per_group
            query = jnp.where(acc == SPARE, 0, base)
            return pieces, base, query

        @pl.when(op == BATCH2)
        def _():
            word = listed()
            absorb([stream(0, 2, word), stream(1, 2, word)])

        @pl.when(op == BATCH1)
        def _():
            word = listed()
            absorb([stream(0, 1, word), stream(1, 1, word)])

        @pl.when(op == TURN)
        def _():
            tables_of(turns_ref)
            turn(q_ref, heads, 0)

        @pl.when(op == DIAGONAL)
        def _():
            absorb(
                [([at(me, CURRENT, g)], g * per_group, g * per_group) for g in range(groups)], True
            )

        @pl.when(op == GUEST_TURN)
        def _():
            send_turns.wait_recv()
            send_q.wait_recv()
            tables_of(guest_turns)
            turn(guest_q, per_group, guest_base)

        @pl.when(op == PACK)
        def _():
            for h in range(per_group):
                part = total[guest_base + h]
                share = part[HEAD_SIZE : HEAD_SIZE + 1]
                back[h] = (part[:HEAD_SIZE] / share).astype(jnp.bfloat16)
                back_stats[0, h : h + 1] = top[guest_base + h]
                back_stats[1, h : h + 1] = share

        @pl.when(op == RETURN)
        def _():
            send_stats.start()
            send_back.start()

        @pl.when(op == PAGES)
        def _():
            pages()

        @pl.when(op == MERGE)
        def _():
            send_stats.wait_recv()
            send_back.wait_recv()
            for h in range(per_group):
                mine, other = top[h], came_stats[0, h : h + 1]
                new = jnp.maximum(mine, other)
                keep = jnp.exp2(mine - new)
                share = came_stats[1, h : h + 1] * jnp.exp2(other - new)
                total[h, :HEAD_SIZE] = (
                    total[h, :HEAD_SIZE] * keep + came[h].astype(jnp.float32) * share
                )
                total[h, HEAD_SIZE : HEAD_SIZE + 1] = (
                    total[h, HEAD_SIZE : HEAD_SIZE + 1] * keep + share
                )

        return carry

    lax.fori_loop(0, length, step, 0)

    for h in range(heads):
        finished = total[h, :HEAD_SIZE] / total[h, HEAD_SIZE : HEAD_SIZE + 1]
        out_ref[:, h * HEAD_SIZE : (h + 1) * HEAD_SIZE] = finished.T.astype(out_ref.dtype)

    def drain(row, carry):
        _, *sent = fields(row)
        for way in (ACROSS, RIGHT, LEFT):

            @pl.when(sent[way] > 0)
            def _():
                remote(way, sent[way] - 1).wait_send()

        return carry

    lax.fori_loop(0, length, drain, 0)

    @pl.when(is_top)
    def _():
        send_turns.wait_send()
        send_q.wait_send()

    @pl.when(is_helper)
    def _():
        send_stats.wait_send()
        send_back.wait_send()


def shards(
    queries, current_keys, current_values, stored_keys, stored_values, remap_table, block_table
):
    tokens, width = queries.shape
    key_width = current_keys.shape[1]
    groups = key_width // HEAD_SIZE
    heads = width // HEAD_SIZE
    per_group = heads // groups
    owners = lax.axis_size("seq")
    length, tables = schedule(owners, groups)
    pieces = owners * KINDS * groups
    blocks = tokens // QBLK
    half_dim = HEAD_SIZE // 2
    frequency = rope_base ** (-2.0 * jnp.arange(half_dim, dtype=jnp.float32) / HEAD_SIZE)
    frequency = jnp.concatenate([frequency, frequency])[None, :]
    bases = remap_table[::-1].reshape(KINDS * blocks, 1).astype(jnp.float32)
    turns = jnp.pad(bases * frequency, ((0, -KINDS * blocks % 8), (0, 0)))
    stored = jnp.stack(
        [
            jnp.stack(
                [
                    jnp.stack([x[:, s, g * HEAD_SIZE : (g + 1) * HEAD_SIZE] for x in (stored_keys, stored_values)])
                    for g in range(groups)
                ]
            )
            for s in range(PRIOR_SEGMENTS)
        ]
    )
    rounds = tokens // PAGE_TOKENS // owners
    here = owners * rounds
    hbm = pl.BlockSpec(memory_space=pltpu.HBM)
    vmem = pl.BlockSpec(memory_space=pltpu.VMEM)
    smem = pl.BlockSpec(memory_space=pltpu.SMEM)
    slots = heads + 2 * per_group
    bf16, f32 = jnp.bfloat16, jnp.float32
    attended, paged = pl.pallas_call(
        functools.partial(kernel, owners, groups, per_group, length, tables),
        out_shape=(
            jax.ShapeDtypeStruct((tokens, width), bf16),
            jax.ShapeDtypeStruct((2, groups, here, PAGE_TOKENS * HEAD_SIZE), bf16),
        ),
        in_specs=[smem, vmem, vmem, hbm, hbm, hbm, hbm],
        out_specs=(vmem, vmem),
        scratch_shapes=[
            pltpu.SMEM((2, length), jnp.int32),
            pltpu.VMEM((tokens, width), bf16),
            pltpu.VMEM((tokens, per_group * HEAD_SIZE), bf16),
            pltpu.VMEM(turns.shape, f32),
            pltpu.VMEM((KINDS, tokens, HEAD_SIZE), f32),
            pltpu.VMEM((KINDS, tokens, HEAD_SIZE), f32),
            pltpu.VMEM((pieces, 2, tokens, HEAD_SIZE), bf16),
            pltpu.VMEM((KINDS, heads + per_group, 2 * HEAD_SIZE, tokens), bf16),
            pltpu.VMEM((slots, 1, tokens), f32),
            pltpu.VMEM((slots, HEAD_SIZE + ONES_ROWS, tokens), f32),
            pltpu.VMEM((2, here * PAGE_TOKENS, key_width), bf16),
            pltpu.VMEM((per_group, HEAD_SIZE, tokens), bf16),
            pltpu.VMEM((2, per_group, tokens), f32),
            pltpu.VMEM((per_group, HEAD_SIZE, tokens), bf16),
            pltpu.VMEM((2, per_group, tokens), f32),
            pltpu.SemaphoreType.DMA((1 + PRIOR_SEGMENTS * groups + 2 * groups,)),
            pltpu.SemaphoreType.DMA((3, pieces)),
            pltpu.SemaphoreType.DMA((pieces,)),
            pltpu.SemaphoreType.DMA((4,)),
            pltpu.SemaphoreType.DMA((4,)),
        ],
        compiler_params=pltpu.CompilerParams(
            collective_id=0, has_side_effects=True, vmem_limit_bytes=56 * 1024 * 1024
        ),
    )(block_table, turns, frequency, queries, stored, current_keys, current_values)
    return (attended, paged[0], paged[1])


def solution(mesh):
    in_specs = (
        P(("groups", "seq"), "head"),
        P(("groups", "seq"), "head"),
        P(("groups", "seq"), "head"),
        P(("groups", "seq"), None, "head"),
        P(("groups", "seq"), None, "head"),
        P(None, ("groups", "seq")),
        P("groups"),
    )
    out_specs = (
        P(("groups", "seq"), "head"),
        P("head", ("groups", "seq"), None),
        P("head", ("groups", "seq"), None),
    )
    return jax.shard_map(shards, mesh=mesh, in_specs=in_specs, out_specs=out_specs, check_vma=False)
```

time: 83.8 us -> 75.6 us (0.902)
  Pallas kernels: 71.6 us -> 64.8 us
  local copies, waits for them, and re-layouts: 9.14 us -> 8.16 us
    pallas_call x1, Pallas kernels: 71.6 us -> 64.8 us  [shards(): pl.pallas_call(functools.partial(kernel, owners, groups, per_group, lengt...]
    squeeze x1, local copies, waits for them, and re-layouts: 0.18 us -> 1.68 us  [shards(): return (attended, paged[0], paged[1])]
    neg x1 -> x0, other arithmetic: 1.45 us -> none  [shards(): sin = jnp.concatenate([-sin, sin], -1)]
    unnamed x15 -> x5, local copies, waits for them, and re-layouts: 5 us -> 3.76 us
    scatter x1 -> x0, local copies, waits for them, and re-layouts: 1.23 us -> none  [shards(): paged = jnp.zeros_like(arranged).at[:, :, target].set(arranged)]
    slice x3 -> x2, local copies, waits for them, and re-layouts: 0.74 us -> 1.92 us  [shards(): x[:, s, g * HEAD_SIZE:(g + 1) * HEAD_SIZE]]
    broadcast_in_dim x2 -> x0, local copies, waits for them, and re-layouts: 0.9 us -> none  [the longest x1 0.76 us: shards(): jnp.repeat(remap_table, QBLK, axis=1)]
    another operation x3 -> x7, other arithmetic: 0.11 us -> 0.96 us  [the longest x3 0.9 us: shards(): jnp.stack([jnp.stack([jnp.stack([x[:, s, g * HEAD_SIZE:(g + 1) * HEAD_SIZ...]
where the time goes in v1:
time: 75.6 us; the launch traced here: 75.3 us
  Pallas kernels  64.8 us (86%)
  local copies, waits for them, and re-layouts  8.16 us (11%)
  other arithmetic  1.64 us (2%)
    pallas_call x1, Pallas kernels, shards(): pl.pallas_call(functools.partial(kernel, owners, groups, per_group, lengt...  64.8 us
    unnamed x5, local copies, waits for them, and re-layouts  3.76 us
    slice x2, local copies, waits for them, and re-layouts, shards(): x[:, s, g * HEAD_SIZE:(g + 1) * HEAD_SIZE]  1.92 us
    squeeze x1, local copies, waits for them, and re-layouts, shards(): return (attended, paged[0], paged[1])  1.68 us

profile of v1, /device:TPU:28, one launch (start us, length us, event | category | flops | bytes accessed | tf_op | source)
XLA Modules:
  0.0 75.3 jit_solution(8517123461302594276)
XLA Ops:
  0.6 0.6 fusion
  1.2 0.0 copy-start.1
  1.2 0.7 copy-done.1
  1.9 0.1 convert_element_type.14
  2.0 0.1 broadcast_multiply_fusion
  2.1 0.6 pad.4.turns_ref
  2.7 1.6 %fusion.1 = (bf16[256,1,128]{2,1,0:T(2,128)(2,1)S(1)}, bf16[256,1,128]{2,1,0:T(2,128)(2,1)S(1)}, bf16[256,1,128]{2,1,0:T(2,128)(2,1)S(1)}, bf16[256,1,128]{2,1,0:T(2,128)(2,1)S(1)}) fusion(bf16[256,2,256]{2,1,0:T(2,128)(2,1)} %param.10), kind=kLoop, calls=%fused_computation.21 | loop fusion | bytes 524288 | tf_op jit(solution)/shard_map/slice | solution.py:682
  4.3 0.0 copy-start
  4.3 0.9 %copy-done = bf16[256,2,256]{2,1,0:T(2,128)(2,1)S(1)} copy-done((bf16[256,2,256]{2,1,0:T(2,128)(2,1)S(1)}, bf16[256,2,256]{2,1,0:T(2,128)(2,1)}, u32[]{:S(2)}) %copy-start) | copy-done | bytes 262168
  5.3 0.4 fusion.2
  5.8 0.8 %pad_maximum_fusion.stored_ref = bf16[2,2,2,256,128]{4,3,2,1,0:T(8,128)(2,1)} fusion(bf16[1,2,2,256,128]{4,3,2,1,0:T(8,128)(2,1)S(1)} %maximum_bitcast_fusion.1, bf16[1,2,2,256,128]{4,3,2,1,0:T(8,128)(2,1)S(1)} %maximum_bitcast_fusion), kind=kLoop, calls=%fused_computation | loop fusion | flops 262144 | bytes 1048576 | tf_op jit(solution)/shard_map/stack | solution.py:678
  6.7 64.8 %shard_map.94 = (bf16[256,1792]{1,0:T(8,128)(2,1)}, bf16[2,2,16,2048]{3,2,1,0:T(8,128)(2,1)}) custom-call(s32[128]{0:T(128)} %table_ref.1, f32[16,128]{1,0:T(8,128)} %pad.4.turns_ref, f32[1,128]{1,0:T(1,128)} %get-tuple-element.17.freq_ref, bf16[256,1792]{1,0:T(8,128)(2,1)} %q_hbm.1, bf16[2,2,2,256,128]{4,3,2,1,0:T(8,128)(2,1)} %pad_maximum_fusion.stored_ref, ...), custom_call_target="tpu_custom_call" | custom-call | tf_op jit(solution)/shard_map/pallas_call | solution.py:696
  71.5 1.7 %slice_bitcast_fusion = (bf16[2,16,2048]{2,1,0:T(8,128)(2,1)}, bf16[2,16,2048]{2,1,0:T(8,128)(2,1)}) fusion(bf16[2,2,16,2048]{3,2,1,0:T(8,128)(2,1)} %get-tuple-element.6), kind=kLoop, calls=%fused_computation.7 | loop fusion | bytes 524288 | tf_op jit(solution)/shard_map/squeeze | solution.py:730
  73.2 2.2 %copy.35 = bf16[256,1792]{1,0:T(8,128)(2,1)} copy(bf16[256,1792]{1,0:T(8,128)(2,1)} %get-tuple-element.30) | data formatting | bytes 1835008
  (13 shorter events, 0.2 us)
Async XLA Ops:
  1.2 0.7 copy-start.1
  4.3 1.0 %copy-start = (bf16[256,2,256]{2,1,0:T(2,128)(2,1)S(1)}, bf16[256,2,256]{2,1,0:T(2,128)(2,1)}, u32[]{:S(2)}) copy-start(bf16[256,2,256]{2,1,0:T(2,128)(2,1)} %param.11) | copy-start | bytes 786436

commit v2 on v1

--- a/solution.py
+++ b/solution.py
@@ -21,6 +21,7 @@
 MESH = pl.DeviceIdType.MESH
 RIGHT, LEFT, ACROSS = 0, 1, 2
 ONES_ROWS = 16
+GRANT = 40 * 1024 * 1024
 
 OWN0, OWN1, GUEST, SPARE = 0, 1, 2, 3
 NOTHING, BATCH2, BATCH1, TURN, DIAGONAL, GUEST_TURN, PACK, RETURN, PAGES, MERGE = range(10)
@@ -167,6 +168,9 @@
         def emit(wait=None, op=NOTHING, pieces=(), accs=()):
             if wait is not None:
                 have.add(wait)
+            if wait is None and op != NOTHING and rows and rows[-1][2] == NOTHING:
+                rows[-1][2:] = [op, list(pieces), list(accs)]
+                return
             rows.append([wait, ready_sends(), op, list(pieces), list(accs)])
             while True:
                 more = ready_sends()
@@ -285,25 +289,23 @@
     for rows in tables:
         words = []
         for wait, sent, op, pieces, accs in rows:
-            first = 0 if wait is None else number(wait) + 1
-            for way in (RIGHT, LEFT, ACROSS):
-                if way in sent:
-                    first += (number(sent[way]) + 1) * FIELD ** (way + 1)
-            second = sum(number(x) * FIELD**k for k, x in enumerate(pieces))
-            third = op + 16 * sum(acc * 4**k for k, acc in enumerate(accs))
-            words.append((first, second, third))
-        words += [(0, 0, 0)] * (length - len(words))
+            first = [0 if wait is None else number(wait) + 1]
+            first += [number(sent[way]) + 1 if way in sent else 0 for way in (RIGHT, LEFT, ACROSS)]
+            listed = sum(number(x) * FIELD**k for k, x in enumerate(pieces))
+            accs = list(accs) + [0] * (2 - len(accs))
+            words.append((first + [op] + accs, listed))
+        words += [([0] * 7, 0)] * (length - len(words))
         packed_tables.append(words)
     return length, packed_tables
 
 
-def kernel(
-    n, groups, per_group, length, tables,
-    table_ref, turns_ref, freq_ref, q_hbm, stored_ref, keys_hbm, values_hbm,
-    out_ref, paged_ref,
-    rows_ref, q_ref, guest_q, guest_turns, cos_ref, sin_ref, held, turned, top, total, raw,
-    back, back_stats, came, came_stats, own_sem, send_sem, recv_sem, side_send, side_recv,
-):
+def kernel(n, groups, per_group, length, tables, table_ref, remap_ref, q_hbm, *refs):
+    sources = [refs[2 * part : 2 * part + 2] for part in range(KINDS)]
+    (
+        out_ref, paged_keys_ref, paged_values_ref,
+        rows_ref, q_ref, turns, guest_q, guest_turns, cos_ref, sin_ref, held, turned, top, total,
+        raw, back, back_stats, came, came_stats, own_sem, send_sem, recv_sem, side_send, side_recv,
+    ) = refs[2 * KINDS :]
     me = lax.axis_index("seq")
     partner = me + 1 - 2 * (me % 2)
     tokens = q_hbm.shape[0]
@@ -320,22 +322,16 @@
         return (j * KINDS + part) * groups + g
 
     own = [pltpu.make_async_copy(q_hbm, q_ref, own_sem.at[0])]
-    for part in range(PRIOR_SEGMENTS):
+    for part in range(KINDS):
         for g in range(groups):
-            own.append(
-                pltpu.make_async_copy(
-                    stored_ref.at[part, g], held.at[at(me, part, g)], own_sem.at[len(own)]
+            for kv, ref in enumerate(sources[part]):
+                own.append(
+                    pltpu.make_async_copy(
+                        ref.at[:, pl.ds(g * HEAD_SIZE, HEAD_SIZE)],
+                        held.at[at(me, part, g), kv],
+                        own_sem.at[len(own)],
+                    )
                 )
-            )
-    for g in range(groups):
-        for kv, ref in enumerate((keys_hbm, values_hbm)):
-            own.append(
-                pltpu.make_async_copy(
-                    ref.at[:, pl.ds(g * HEAD_SIZE, HEAD_SIZE)],
-                    held.at[at(me, CURRENT, g), kv],
-                    own_sem.at[len(own)],
-                )
-            )
     for copy in own:
         copy.start()
     barrier = pltpu.get_barrier_semaphore()
@@ -349,13 +345,32 @@
     def _():
         pl.semaphore_signal(barrier, inc=1, device_id={"seq": me - 2}, device_id_type=MESH)
 
+    lane = lax.broadcasted_iota(jnp.int32, (1, HEAD_SIZE), 1)
+    power = (lane % (HEAD_SIZE // 2)).astype(jnp.float32) * (-2.0 * math.log2(rope_base) / HEAD_SIZE)
+    frequency = jnp.exp2(power)
+    for part in range(KINDS):
+        for b in range(blocks):
+            base = remap_ref[KINDS - 1 - part, b].astype(jnp.float32)
+            turns[part * blocks + b : part * blocks + b + 1] = base * frequency
+    if turns.shape[0] > KINDS * blocks:
+        rest = turns.shape[0] - KINDS * blocks
+        turns[KINDS * blocks :] = jnp.zeros((rest, HEAD_SIZE), jnp.float32)
+
     for d in range(n):
 
         @pl.when(me == d)
         def _():
-            for k, words in enumerate(tables[d]):
-                rows_ref[0, k] = words[0]
-                rows_ref[1, k] = words[2]
+            for k, (words, _) in enumerate(tables[d]):
+                for c, word in enumerate(words):
+                    rows_ref[c, k] = word * per_group if c > 4 else word
+
+    top[...] = jnp.full(top.shape, masked_value, jnp.float32)
+
+    def clear(h, carry):
+        total[h] = jnp.zeros(total.shape[1:], jnp.float32)
+        return carry
+
+    lax.fori_loop(0, total.shape[0], clear, 0)
 
     expected = 1 + has_right.astype(jnp.int32) + has_left.astype(jnp.int32)
     pl.semaphore_wait(barrier, expected)
@@ -373,7 +388,7 @@
     down = jnp.maximum(me - 2, 0)
     up = jnp.minimum(me + 2, n - 1)
     send_q = side(0, q_ref.at[:, pl.ds(0, width)], guest_q, down)
-    send_turns = side(1, turns_ref, guest_turns, down)
+    send_turns = side(1, turns, guest_turns, down)
     send_back = side(2, back, came, up)
     send_stats = side(3, back_stats, came_stats, up)
 
@@ -398,13 +413,9 @@
             device_id_type=MESH,
         )
 
-    def fields(row):
-        word = rows_ref[0, row]
-        return [word // FIELD**k % FIELD for k in range(4)]
-
     def tables_of(ref):
         rows = lax.broadcasted_iota(jnp.int32, (QBLK, HEAD_SIZE), 0).astype(jnp.float32)
-        angle = rows * freq_ref[...]
+        angle = rows * frequency
         near_cos, near_sin = jnp.cos(angle), jnp.sin(angle)
         far = ref[...]
         far_cos, far_sin = jnp.cos(far), jnp.sin(far)
@@ -433,14 +444,6 @@
             return carry
 
         lax.fori_loop(0, KINDS, one, 0)
-
-    top[...] = jnp.full(top.shape, masked_value, jnp.float32)
-
-    def clear(h, carry):
-        total[h] = jnp.zeros(total.shape[1:], jnp.float32)
-        return carry
-
-    lax.fori_loop(0, total.shape[0], clear, 0)
 
     def absorb(streams, causal=False):
         ready = []
@@ -523,61 +526,66 @@
             moved = moved.astype(jnp.bfloat16)
             for g in range(groups):
                 for t in range(PAGE_TOKENS):
-                    paged_ref[kv, g, :, t * HEAD_SIZE : (t + 1) * HEAD_SIZE] = moved[
+                    (paged_keys_ref, paged_values_ref)[kv][g, :, t * HEAD_SIZE : (t + 1) * HEAD_SIZE] = moved[
                         t * here : (t + 1) * here, g * HEAD_SIZE : (g + 1) * HEAD_SIZE
                     ]
 
     guest_base = heads
     spare_base = heads + per_group
 
+    listed = []
+    for r in range(length):
+        choice = None
+        for d in range(n):
+            value = tables[d][r][1]
+            if value:
+                choice = value if choice is None else jnp.where(me == d, value, choice)
+        if choice is not None:
+            listed.append((r, choice))
+
     def step(row, carry):
-        wait, *sent = fields(row)
+        wait, right, left, across, op, first, second = [rows_ref[c, row] for c in range(7)]
 
         @pl.when(wait > 0)
         def _():
             remote(RIGHT, wait - 1).wait_recv()
 
-        for way in (ACROSS, RIGHT, LEFT):
-
-            @pl.when(sent[way] > 0)
-            def _():
-                remote(way, sent[way] - 1).start()
-
-        third = rows_ref[1, row]
-        op = third % 16
-
-        def listed():
+        @pl.when(right + left + across > 0)
+        def _():
+            for way, sent in ((ACROSS, across), (RIGHT, right), (LEFT, left)):
+
+                @pl.when(sent > 0)
+                def _():
+                    remote(way, sent - 1).start()
+
+        def streams(size):
             word = jnp.int32(0)
-            for r in range(length):
-                choice = None
-                for d in range(n):
-                    value = tables[d][r][1]
-                    if value:
-                        choice = value if choice is None else jnp.where(me == d, value, choice)
-                if choice is not None:
-                    word = jnp.where(row == r, choice, word)
-            return word
-
-        def stream(k, size, second):
-            acc = third // (16 * 4**k) % 4
-            pieces = [second // FIELD ** (k * size + i) % FIELD for i in range(size)]
-            base = acc * per_group
-            query = jnp.where(acc == SPARE, 0, base)
-            return pieces, base, query
+            for r, choice in listed:
+                word = jnp.where(row == r, choice, word)
+            some = []
+            for k, base in enumerate((first, second)):
+                pieces = [word // FIELD ** (k * size + i) % FIELD for i in range(size)]
+                some.append((pieces, base, jnp.where(base == spare_base, 0, base)))
+            return some
 
         @pl.when(op == BATCH2)
         def _():
-            word = listed()
-            absorb([stream(0, 2, word), stream(1, 2, word)])
+            absorb(streams(2))
 
         @pl.when(op == BATCH1)
         def _():
-            word = listed()
-            absorb([stream(0, 1, word), stream(1, 1, word)])
-
+            absorb(streams(1))
+
+        @pl.when(op > BATCH1)
+        def _():
+            others(op)
+
+        return carry
+
+    def others(op):
         @pl.when(op == TURN)
         def _():
-            tables_of(turns_ref)
+            tables_of(turns)
             turn(q_ref, heads, 0)
 
         @pl.when(op == DIAGONAL)
@@ -627,25 +635,20 @@
                     total[h, HEAD_SIZE : HEAD_SIZE + 1] * keep + share
                 )
 
-        return carry
-
     lax.fori_loop(0, length, step, 0)
 
     for h in range(heads):
         finished = total[h, :HEAD_SIZE] / total[h, HEAD_SIZE : HEAD_SIZE + 1]
         out_ref[:, h * HEAD_SIZE : (h + 1) * HEAD_SIZE] = finished.T.astype(out_ref.dtype)
 
-    def drain(row, carry):
-        _, *sent = fields(row)
-        for way in (ACROSS, RIGHT, LEFT):
-
-            @pl.when(sent[way] > 0)
-            def _():
-                remote(way, sent[way] - 1).wait_send()
-
-        return carry
-
-    lax.fori_loop(0, length, drain, 0)
+    for d in range(n):
+
+        @pl.when(me == d)
+        def _():
+            for words, _ in tables[d]:
+                for way in (RIGHT, LEFT, ACROSS):
+                    if words[1 + way]:
+                        remote(way, words[1 + way] - 1).wait_send()
 
     @pl.when(is_top)
     def _():
@@ -656,6 +659,17 @@
     def _():
         send_stats.wait_send()
         send_back.wait_send()
+
+
+def finish(*refs):
+    half = len(refs) // 3
+    copies = [
+        pltpu.make_async_copy(refs[k], refs[half + k], refs[2 * half + k]) for k in range(half)
+    ]
+    for copy in copies:
+        copy.start()
+    for copy in copies:
+        copy.wait()
 
 
 def shards(
@@ -670,42 +684,31 @@
     length, tables = schedule(owners, groups)
     pieces = owners * KINDS * groups
     blocks = tokens // QBLK
-    half_dim = HEAD_SIZE // 2
-    frequency = rope_base ** (-2.0 * jnp.arange(half_dim, dtype=jnp.float32) / HEAD_SIZE)
-    frequency = jnp.concatenate([frequency, frequency])[None, :]
-    bases = remap_table[::-1].reshape(KINDS * blocks, 1).astype(jnp.float32)
-    turns = jnp.pad(bases * frequency, ((0, -KINDS * blocks % 8), (0, 0)))
-    stored = jnp.stack(
-        [
-            jnp.stack(
-                [
-                    jnp.stack([x[:, s, g * HEAD_SIZE : (g + 1) * HEAD_SIZE] for x in (stored_keys, stored_values)])
-                    for g in range(groups)
-                ]
-            )
-            for s in range(PRIOR_SEGMENTS)
-        ]
-    )
+    sources = [x[:, s, :] for s in range(PRIOR_SEGMENTS) for x in (stored_keys, stored_values)]
+    sources += [current_keys, current_values]
     rounds = tokens // PAGE_TOKENS // owners
     here = owners * rounds
     hbm = pl.BlockSpec(memory_space=pltpu.HBM)
     vmem = pl.BlockSpec(memory_space=pltpu.VMEM)
     smem = pl.BlockSpec(memory_space=pltpu.SMEM)
     slots = heads + 2 * per_group
+    turn_rows = -(-KINDS * blocks // 8) * 8
     bf16, f32 = jnp.bfloat16, jnp.float32
-    attended, paged = pl.pallas_call(
+    results = pl.pallas_call(
         functools.partial(kernel, owners, groups, per_group, length, tables),
         out_shape=(
             jax.ShapeDtypeStruct((tokens, width), bf16),
-            jax.ShapeDtypeStruct((2, groups, here, PAGE_TOKENS * HEAD_SIZE), bf16),
+            jax.ShapeDtypeStruct((groups, here, PAGE_TOKENS * HEAD_SIZE), bf16),
+            jax.ShapeDtypeStruct((groups, here, PAGE_TOKENS * HEAD_SIZE), bf16),
         ),
-        in_specs=[smem, vmem, vmem, hbm, hbm, hbm, hbm],
-        out_specs=(vmem, vmem),
+        in_specs=[smem, smem, hbm] + [hbm] * len(sources),
+        out_specs=(vmem, vmem, vmem),
         scratch_shapes=[
-            pltpu.SMEM((2, length), jnp.int32),
+            pltpu.SMEM((7, length), jnp.int32),
             pltpu.VMEM((tokens, width), bf16),
+            pltpu.VMEM((turn_rows, HEAD_SIZE), f32),
             pltpu.VMEM((tokens, per_group * HEAD_SIZE), bf16),
-            pltpu.VMEM(turns.shape, f32),
+            pltpu.VMEM((turn_rows, HEAD_SIZE), f32),
             pltpu.VMEM((KINDS, tokens, HEAD_SIZE), f32),
             pltpu.VMEM((KINDS, tokens, HEAD_SIZE), f32),
             pltpu.VMEM((pieces, 2, tokens, HEAD_SIZE), bf16),
@@ -717,17 +720,24 @@
             pltpu.VMEM((2, per_group, tokens), f32),
             pltpu.VMEM((per_group, HEAD_SIZE, tokens), bf16),
             pltpu.VMEM((2, per_group, tokens), f32),
-            pltpu.SemaphoreType.DMA((1 + PRIOR_SEGMENTS * groups + 2 * groups,)),
+            pltpu.SemaphoreType.DMA((1 + 2 * KINDS * groups,)),
             pltpu.SemaphoreType.DMA((3, pieces)),
             pltpu.SemaphoreType.DMA((pieces,)),
             pltpu.SemaphoreType.DMA((4,)),
             pltpu.SemaphoreType.DMA((4,)),
         ],
         compiler_params=pltpu.CompilerParams(
-            collective_id=0, has_side_effects=True, vmem_limit_bytes=56 * 1024 * 1024
+            collective_id=0, has_side_effects=True, vmem_limit_bytes=GRANT
         ),
-    )(block_table, turns, frequency, queries, stored, current_keys, current_values)
-    return (attended, paged[0], paged[1])
+    )(block_table, remap_table, queries, *sources)
+    return pl.pallas_call(
+        finish,
+        out_shape=tuple(jax.ShapeDtypeStruct(x.shape, x.dtype) for x in results),
+        in_specs=[vmem] * 3,
+        out_specs=(hbm,) * 3,
+        scratch_shapes=[pltpu.SemaphoreType.DMA] * 3,
+        compiler_params=pltpu.CompilerParams(vmem_limit_bytes=8 * 1024 * 1024),
+    )(*results)
 
 
 def solution(mesh):

time: 75.6 us -> 62 us (0.82)
  Pallas kernels: 64.8 us -> 57.4 us
  local copies, waits for them, and re-layouts: 8.16 us -> 3.77 us
  other arithmetic: 1.64 us -> 0 us
    pallas_call x1, Pallas kernels: 64.8 us -> 56.3 us  [shards(): pl.pallas_call(functools.partial(kernel, owners, groups, per_group, lengt...]
    unnamed x5 -> x12, local copies, waits for them, and re-layouts: 3.76 us -> 1.84 us
    squeeze x1 -> x2, local copies, waits for them, and re-layouts: 1.68 us -> 0.08 us  [shards(): x[:, s, :]]
    pallas_call x0 -> x1, Pallas kernels: none -> 1.03 us  [shards(): pl.pallas_call(finish, out_shape=tuple((jax.ShapeDtypeStruct(x.shape, x.d...]
    another operation x7 -> x0, other arithmetic: 0.96 us -> none  [the longest x3 0.9 us: shards(): jnp.stack([jnp.stack([jnp.stack([x[:, s, g * HEAD_SIZE:(g + 1) * HEAD_SIZ...]
where the time goes in v2:
time: 62 us; the launch traced here: 61.8 us
  Pallas kernels  57.4 us (93%)
  local copies, waits for them, and re-layouts  3.77 us (6%)
  between operations  0.7 us (1%)
    pallas_call x1, Pallas kernels, shards(): pl.pallas_call(functools.partial(kernel, owners, groups, per_group, lengt...  56.3 us
    slice x2, local copies, waits for them, and re-layouts, shards(): x[:, s, :]  1.85 us
    unnamed x12, local copies, waits for them, and re-layouts  1.84 us

profile of v2, /device:TPU:28, one launch (start us, length us, event | category | flops | bytes accessed | tf_op | source)
XLA Modules:
  0.0 61.8 jit_solution(16140206232952152878)
XLA Ops:
  0.6 1.5 %fusion.1 = (bf16[256,1,256]{2,1,0:T(2,128)(2,1)S(1)}, bf16[256,1,256]{2,1,0:T(2,128)(2,1)S(1)}) fusion(bf16[256,2,256]{2,1,0:T(2,128)(2,1)} %param.10), kind=kLoop, calls=%fused_computation.5 | loop fusion | bytes 524288 | tf_op jit(solution)/shard_map/slice | solution.py:687
  2.1 0.0 copy-start.5
  2.2 0.9 %copy-done.5 = bf16[256,2,256]{2,1,0:T(2,128)(2,1)S(1)} copy-done((bf16[256,2,256]{2,1,0:T(2,128)(2,1)S(1)}, bf16[256,2,256]{2,1,0:T(2,128)(2,1)}, u32[]{:S(2)}) %copy-start.5) | copy-done | bytes 262168
  3.1 0.0 copy-start
  3.1 0.4 fusion
  3.4 0.0 copy-start.1
  3.5 0.0 copy-start.2
  3.5 0.0 copy-start.3
  3.5 0.0 copy-start.4
  3.5 0.7 %copy-done = bf16[256,1792]{1,0:T(8,128)(2,1)S(1)} copy-done((bf16[256,1792]{1,0:T(8,128)(2,1)S(1)}, bf16[256,1792]{1,0:T(8,128)(2,1)}, u32[]{:S(2)}) %copy-start) | copy-done | bytes 917528
  4.2 0.2 copy-done.1
  4.4 0.0 copy-done.2
  4.5 0.0 copy-done.3
  4.5 0.0 copy-done.4
  4.5 56.3 %shard_map.94 = (bf16[256,1792]{1,0:T(8,128)(2,1)S(1)}, bf16[2,16,2048]{2,1,0:T(8,128)(2,1)S(1)}, bf16[2,16,2048]{2,1,0:T(8,128)(2,1)S(1)}) custom-call(s32[128]{0:T(128)S(1)} %copy-done.4, s32[3,4]{1,0:T(4,128)S(1)} %copy-done.3, bf16[256,1792]{1,0:T(8,128)(2,1)S(1)} %copy-done, bf16[256,256]{1,0:T(8,128)(2,1)S(1)} %get-tuple-element.14.refs_0_, ...), custom_call_target="tpu_custom_call" | custom-call | tf_op jit(solution)/shard_map/pallas_call | solution.py:697
  60.8 1.0 %shard_map.95 = (bf16[256,1792]{1,0:T(8,128)(2,1)}, bf16[2,16,2048]{2,1,0:T(8,128)(2,1)}, bf16[2,16,2048]{2,1,0:T(8,128)(2,1)}) custom-call(bf16[256,1792]{1,0:T(8,128)(2,1)S(1)} %get-tuple-element.6.refs_0_, bf16[2,16,2048]{2,1,0:T(8,128)(2,1)S(1)} %get-tuple-element.7.refs_1_, bf16[2,16,2048]{2,1,0:T(8,128)(2,1)S(1)} %get-tuple-element.8.refs_2_), custom_call_target="tpu_custom_call" | custom-call | tf_op jit(solution)/shard_map/pallas_call | solution.py:733
  (2 shorter events, 0.1 us)
Async XLA Ops:
  2.1 1.0 %copy-start.5 = (bf16[256,2,256]{2,1,0:T(2,128)(2,1)S(1)}, bf16[256,2,256]{2,1,0:T(2,128)(2,1)}, u32[]{:S(2)}) copy-start(bf16[256,2,256]{2,1,0:T(2,128)(2,1)} %param.11) | copy-start | bytes 786436
  3.1 1.2 %copy-start = (bf16[256,1792]{1,0:T(8,128)(2,1)S(1)}, bf16[256,1792]{1,0:T(8,128)(2,1)}, u32[]{:S(2)}) copy-start(bf16[256,1792]{1,0:T(8,128)(2,1)} %q_hbm.1) | copy-start | bytes 2752516
  3.4 1.0 %copy-start.1 = (bf16[256,256]{1,0:T(8,128)(2,1)S(1)}, bf16[256,256]{1,0:T(8,128)(2,1)}, u32[]{:S(2)}) copy-start(bf16[256,256]{1,0:T(8,128)(2,1)} %refs_4_.1) | copy-start | bytes 393220
  3.5 1.0 %copy-start.2 = (bf16[256,256]{1,0:T(8,128)(2,1)S(1)}, bf16[256,256]{1,0:T(8,128)(2,1)}, u32[]{:S(2)}) copy-start(bf16[256,256]{1,0:T(8,128)(2,1)} %refs_5_.1) | copy-start | bytes 393220
  3.5 0.9 %copy-start.3 = (s32[3,4]{1,0:T(4,128)S(1)}, s32[3,4]{1,0:T(4,128)}, u32[]{:S(2)}) copy-start(s32[3,4]{1,0:T(4,128)} %remap_ref.1) | copy-start | bytes 148
  3.5 0.9 %copy-start.4 = (s32[128]{0:T(128)S(1)}, s32[128]{0:T(128)}, u32[]{:S(2)}) copy-start(s32[128]{0:T(128)} %table_ref.1) | copy-start | bytes 1540

commit v3 on v2

--- a/solution.py
+++ b/solution.py
@@ -21,7 +21,7 @@
 MESH = pl.DeviceIdType.MESH
 RIGHT, LEFT, ACROSS = 0, 1, 2
 ONES_ROWS = 16
-GRANT = 40 * 1024 * 1024
+GRANT = 60 * 1024 * 1024
 
 OWN0, OWN1, GUEST, SPARE = 0, 1, 2, 3
 NOTHING, BATCH2, BATCH1, TURN, DIAGONAL, GUEST_TURN, PACK, RETURN, PAGES, MERGE = range(10)
@@ -300,12 +300,12 @@
 
 
 def kernel(n, groups, per_group, length, tables, table_ref, remap_ref, q_hbm, *refs):
-    sources = [refs[2 * part : 2 * part + 2] for part in range(KINDS)]
+    stored, current = refs[:2], refs[2:4]
     (
         out_ref, paged_keys_ref, paged_values_ref,
-        rows_ref, q_ref, turns, guest_q, guest_turns, cos_ref, sin_ref, held, turned, top, total,
+        rows_ref, q_ref, mixed, turns, guest_q, guest_turns, cos_ref, sin_ref, held, turned, top, total,
         raw, back, back_stats, came, came_stats, own_sem, send_sem, recv_sem, side_send, side_recv,
-    ) = refs[2 * KINDS :]
+    ) = refs[4:]
     me = lax.axis_index("seq")
     partner = me + 1 - 2 * (me % 2)
     tokens = q_hbm.shape[0]
@@ -322,16 +322,17 @@
         return (j * KINDS + part) * groups + g
 
     own = [pltpu.make_async_copy(q_hbm, q_ref, own_sem.at[0])]
-    for part in range(KINDS):
-        for g in range(groups):
-            for kv, ref in enumerate(sources[part]):
-                own.append(
-                    pltpu.make_async_copy(
-                        ref.at[:, pl.ds(g * HEAD_SIZE, HEAD_SIZE)],
-                        held.at[at(me, part, g), kv],
-                        own_sem.at[len(own)],
-                    )
+    for kv in range(2):
+        own.append(pltpu.make_async_copy(stored[kv], mixed.at[kv], own_sem.at[len(own)]))
+    for g in range(groups):
+        for kv in range(2):
+            own.append(
+                pltpu.make_async_copy(
+                    current[kv].at[:, pl.ds(g * HEAD_SIZE, HEAD_SIZE)],
+                    held.at[at(me, CURRENT, g), kv],
+                    own_sem.at[len(own)],
                 )
+            )
     for copy in own:
         copy.start()
     barrier = pltpu.get_barrier_semaphore()
@@ -364,6 +365,14 @@
                 for c, word in enumerate(words):
                     rows_ref[c, k] = word * per_group if c > 4 else word
 
+    for kv in range(2):
+        own[1 + kv].wait()
+        for part in range(PRIOR_SEGMENTS):
+            for g in range(groups):
+                held[at(me, part, g), kv] = mixed[
+                    kv, :, part, g * HEAD_SIZE : (g + 1) * HEAD_SIZE
+                ]
+
     top[...] = jnp.full(top.shape, masked_value, jnp.float32)
 
     def clear(h, carry):
@@ -399,7 +408,7 @@
         send_turns.start()
         send_q.start()
 
-    for copy in own[1:]:
+    for copy in own[3:]:
         copy.wait()
 
     def remote(way, piece):
@@ -684,8 +693,6 @@
     length, tables = schedule(owners, groups)
     pieces = owners * KINDS * groups
     blocks = tokens // QBLK
-    sources = [x[:, s, :] for s in range(PRIOR_SEGMENTS) for x in (stored_keys, stored_values)]
-    sources += [current_keys, current_values]
     rounds = tokens // PAGE_TOKENS // owners
     here = owners * rounds
     hbm = pl.BlockSpec(memory_space=pltpu.HBM)
@@ -697,15 +704,16 @@
     results = pl.pallas_call(
         functools.partial(kernel, owners, groups, per_group, length, tables),
         out_shape=(
-            jax.ShapeDtypeStruct((tokens, width), bf16),
-            jax.ShapeDtypeStruct((groups, here, PAGE_TOKENS * HEAD_SIZE), bf16),
-            jax.ShapeDtypeStruct((groups, here, PAGE_TOKENS * HEAD_SIZE), bf16),
+            pltpu.VMEM((tokens, width), bf16),
+            pltpu.VMEM((groups, here, PAGE_TOKENS * HEAD_SIZE), bf16),
+            pltpu.VMEM((groups, here, PAGE_TOKENS * HEAD_SIZE), bf16),
         ),
-        in_specs=[smem, smem, hbm] + [hbm] * len(sources),
+        in_specs=[smem, smem] + [hbm] * 5,
         out_specs=(vmem, vmem, vmem),
         scratch_shapes=[
             pltpu.SMEM((7, length), jnp.int32),
             pltpu.VMEM((tokens, width), bf16),
+            pltpu.VMEM((2, tokens, PRIOR_SEGMENTS, key_width), bf16),
             pltpu.VMEM((turn_rows, HEAD_SIZE), f32),
             pltpu.VMEM((tokens, per_group * HEAD_SIZE), bf16),
             pltpu.VMEM((turn_rows, HEAD_SIZE), f32),
@@ -720,7 +728,7 @@
             pltpu.VMEM((2, per_group, tokens), f32),
             pltpu.VMEM((per_group, HEAD_SIZE, tokens), bf16),
             pltpu.VMEM((2, per_group, tokens), f32),
-            pltpu.SemaphoreType.DMA((1 + 2 * KINDS * groups,)),
+            pltpu.SemaphoreType.DMA((3 + 2 * groups,)),
             pltpu.SemaphoreType.DMA((3, pieces)),
             pltpu.SemaphoreType.DMA((pieces,)),
             pltpu.SemaphoreType.DMA((4,)),
@@ -729,7 +737,7 @@
         compiler_params=pltpu.CompilerParams(
             collective_id=0, has_side_effects=True, vmem_limit_bytes=GRANT
         ),
-    )(block_table, remap_table, queries, *sources)
+    )(block_table, remap_table, queries, stored_keys, stored_values, current_keys, current_values)
     return pl.pallas_call(
         finish,
         out_shape=tuple(jax.ShapeDtypeStruct(x.shape, x.dtype) for x in results),

time: 62 us -> 59.6 us (0.961)
  local copies, waits for them, and re-layouts: 3.77 us -> 0 us
  Pallas kernels: 57.4 us -> 58.8 us
    slice x2 -> x0, local copies, waits for them, and re-layouts: 1.85 us -> none  [shards(): x[:, s, :]]
    unnamed x12 -> x0, local copies, waits for them, and re-layouts: 1.84 us -> none
    pallas_call x1, Pallas kernels: 56.3 us -> 57.8 us  [shards(): pl.pallas_call(functools.partial(kernel, owners, groups, per_group, lengt...]
where the time goes in v3:
time: 59.6 us; the launch traced here: 59.5 us
  Pallas kernels  58.8 us (99%)
  between operations  0.64 us (1%)
    pallas_call x1, Pallas kernels, shards(): pl.pallas_call(functools.partial(kernel, owners, groups, per_group, lengt...  57.8 us

profile of v3, /device:TPU:28, one launch (start us, length us, event | category | flops | bytes accessed | tf_op | source)
XLA Modules:
  0.0 59.5 jit_solution(17985088256858059802)
XLA Ops:
  0.6 57.8 %shard_map.94 = (bf16[256,1792]{1,0:T(8,128)(2,1)S(1)}, bf16[2,16,2048]{2,1,0:T(8,128)(2,1)S(1)}, bf16[2,16,2048]{2,1,0:T(8,128)(2,1)S(1)}) custom-call(s32[128]{0:T(128)} %table_ref.1, s32[3,4]{1,0:T(4,128)} %remap_ref.1, bf16[256,1792]{1,0:T(8,128)(2,1)} %q_hbm.1, bf16[256,2,256]{2,1,0:T(2,128)(2,1)} %refs_0_.1, bf16[256,2,256]{2,1,0:T(2,128)(2,1)} %refs_1_.1, ...), custom_call_target="tpu_custom_call" | custom-call | tf_op jit(solution)/shard_map/pallas_call | solution.py:704
  58.4 1.0 %shard_map.95 = (bf16[256,1792]{1,0:T(8,128)(2,1)}, bf16[2,16,2048]{2,1,0:T(8,128)(2,1)}, bf16[2,16,2048]{2,1,0:T(8,128)(2,1)}) custom-call(bf16[256,1792]{1,0:T(8,128)(2,1)S(1)} %get-tuple-element.6.refs_0_, bf16[2,16,2048]{2,1,0:T(8,128)(2,1)S(1)} %get-tuple-element.7.refs_1_, bf16[2,16,2048]{2,1,0:T(8,128)(2,1)S(1)} %get-tuple-element.8.refs_2_), custom_call_target="tpu_custom_call" | custom-call | tf_op jit(solution)/shard_map/pallas_call | solution.py:741
